TPU v7x, 32 devices: a 4x4x1 block of a 4x4x8 slice. The times are simulated.
32 devices in a mesh: dp: 1 (over z), ri: 4 (over y), co: 4 (over x), ro: 2 (over core).
Axes of the slice: x: 4, y: 4, z: 1, core: 2. Of those that a mesh axis runs over, the one named last changes fastest.
The devices are a block of a 4x4x8 slice.
Arguments:
- act_in: bfloat16 [32768, 4096], P(('dp', 'ro', 'ri'), 'co')
- weight: bfloat16 [4096, 14336], P(('ro', 'ri'), 'co')
Outputs:
- output: bfloat16 [32768, 14336], P(('dp', 'ro', 'ri', 'co'))
All inputs are finite; a program needn't handle non-finite values.
Results may differ from a plain program's by a relative error of at most 0.001.
Values are sent between devices in bfloat16 or wider.
A program may use at most 768 MiB of HBM per device.

v0:
```python
import jax
import jax.numpy as jnp
from jax import lax
from jax.sharding import PartitionSpec as P


def solution(mesh):
    def local_block(act_blk, weight_blk):
        act_rows = lax.all_gather(act_blk, "co", axis=1, tiled=True)
        weight_cols = lax.all_gather(weight_blk, ("ro", "ri"), axis=0, tiled=True)
        block_out = jnp.dot(act_rows, weight_cols, preferred_element_type=jnp.float32).astype(jnp.bfloat16)
        return lax.all_to_all(block_out, "co", 0, 1, tiled=True)

    return jax.shard_map(
        local_block,
        mesh=mesh,
        in_specs=(P(("dp", "ro", "ri"), "co"), P(("ro", "ri"), "co")),
        out_specs=P(("dp", "ro", "ri", "co"), None),
        check_vma=False,
    )
```

profile of v0, /device:TPU:97, one launch (start us, length us, event | category | flops | bytes accessed | tf_op | source)
XLA Modules:
  0.0 938.5 jit_solution(7706314303438073789)
XLA Ops:
  6.5 0.0 all-gather.3.cloned.1.call-start
  6.6 0.7 all-gather.3.cloned.1.call-update
  7.3 0.1 all-gather.5.cloned.1.call-start
  7.4 0.7 all-gather.5.cloned.1.call-update
  8.1 296.2 %all-gather.3.cloned.1.call-done = bf16[4096,4096]{1,0:T(8,128)(2,1)} async-done(((bf16[4096,1024]{1,0:T(8,128)(2,1)}), bf16[4096,4096]{1,0:T(8,128)(2,1)}) %all-gather.3.cloned.1.call-update) | async-done | bytes 33554448 | tf_op jit(solution)/shard_map/all_gather | solution.py:9
  304.3 139.5 %all-gather.5.cloned.1.call-done = bf16[4096,3584]{1,0:T(8,128)(2,1)} async-done(((bf16[512,3584]{1,0:T(8,128)(2,1)}), bf16[4096,3584]{1,0:T(8,128)(2,1)}) %all-gather.5.cloned.1.call-update) | async-done | bytes 29360144 | tf_op jit(solution)/shard_map/all_gather | solution.py:10
  443.8 132.9 %convolution_convert_fusion = bf16[4096,3584]{1,0:T(8,128)(2,1)} fusion(bf16[4096,4096]{1,0:T(8,128)(2,1)} %all-gather.3.cloned.1.call-done, bf16[4096,3584]{1,0:T(8,128)(2,1)} %all-gather.5.cloned.1.call-done), kind=kOutput, calls=%fused_computation | convolution fusion | flops 120273764352 | bytes 92274688 | tf_op jit(solution)/shard_map/dot_general | solution.py:11
  576.7 334.5 %all_to_all.19 = bf16[4,1024,3584]{2,1,0:T(8,128)(2,1)} all-to-all(bf16[4,1024,3584]{2,1,0:T(8,128)(2,1)} %bitcast.7), channel_id=1, replica_groups=mesh['dp'=1,'ri'=4,'co'=4,'ro'=2] {'co'}, dimensions={0} | all-to-all | bytes 58720256 | tf_op jit(solution)/shard_map/all_to_all | solution.py:12
  911.2 20.4 %copy.4 = bf16[4,128,8,3584]{3,2,0,1:T(8,128)(2,1)} copy(bf16[4,128,8,3584]{3,2,1,0:T(8,128)(2,1)} %bitcast.6) | data formatting | bytes 58720256 | tf_op jit(solution)/shard_map/all_to_all | solution.py:12
Async XLA Ops:
  6.5 297.8 %all-gather.3.cloned.1.call-start = ((), (), s32[]{:S(2)}) async-start(), calls=%async_computation.1 | async-start | bytes 41943040 | tf_op jit(solution)/shard_map/all_gather | solution.py:9
  7.3 436.5 %all-gather.5.cloned.1.call-start = ((), (), s32[]{:S(2)}) async-start(), calls=%async_computation.2 | async-start | bytes 33030144 | tf_op jit(solution)/shard_map/all_gather | solution.py:10
Sparse Core Ops, SparseCore 0:
  8.9 295.3 all-gather.2
  305.9 137.8 all-gather.4
where the time goes:
time: 939 us; the launch traced here: 938 us
  waiting for transfers between devices  437 us (47%)
  blocking collectives  335 us (36%)
  matrix products  133 us (14%)
  local copies, waits for them, and re-layouts  20.4 us (2%)
  between operations  13.4 us (1%)
    all_to_all x1, blocking collectives, local_block(): return lax.all_to_all(block_out, 'co', 0, 1, tiled=True)  335 us
    all_gather x1, waiting for transfers between devices, local_block(): act_rows = lax.all_gather(act_blk, 'co', axis=1, tiled=True)  296 us
    all_gather x1, waiting for transfers between devices, local_block(): weight_cols = lax.all_gather(weight_blk, ('ro', 'ri'), axis=0, tiled=True)  139 us
    dot_general x1, matrix products, local_block(): jnp.dot(act_rows, weight_cols, preferred_element_type=jnp.float32)  133 us
    all_to_all x1, local copies, waits for them, and re-layouts, local_block(): return lax.all_to_all(block_out, 'co', 0, 1, tiled=True)  20.4 us
  transfers between devices with their start and end apart: 2, of which 2 were waited for; matrix products, arithmetic and copies ran while one was open for 0% of the time, Pallas kernels for 0%

commit v1 on v0

v1 whole, which is shorter than its diff:
```python
import functools

import jax
import jax.numpy as jnp
from jax import lax
from jax.experimental import pallas as pl
from jax.experimental.pallas import tpu as pltpu
from jax.sharding import PartitionSpec as P

MESH = pl.DeviceIdType.MESH
LANES = 128
A_PIECES = 8
P1L, P1R, P1O, P2L, P2R, P2O, Q1L, Q1R, Q1O, Q2L, Q2R, Q2O, DIE = range(13)


def kernel(dims, act, w, out, g, a_v, w_v, b_v, c_v, rsem, ssem, a_rsem, a_ssem, lsem, bsem, csem):
    nx, ny = dims
    kb, wcols = w.shape
    n = wcols // LANES
    full = n // 4
    half = kb // 2
    rows, kd = a_v.shape
    acols = kd // nx
    apiece = rows // A_PIECES

    x, y, c = lax.axis_index("co"), lax.axis_index("ri"), lax.axis_index("ro")
    xl, xr, xo = lax.rem(x + nx - 1, nx), lax.rem(x + 1, nx), lax.rem(x + 2, nx)
    yl, yr = lax.rem(y + ny - 1, ny), lax.rem(y + 1, ny)

    barrier = pltpu.get_barrier_semaphore()
    peers = [{"co": xl}, {"co": xr}, {"co": xo}, {"ri": yl}, {"ri": yr}, {"ro": 1 - c}]
    for peer in peers:
        pl.semaphore_signal(barrier, inc=1, device_id=peer, device_id_type=MESH)
    pl.semaphore_wait(barrier, len(peers))

    def remote(src, dst, kind, j, dev):
        return pltpu.make_async_remote_copy(
            src_ref=src, dst_ref=dst, send_sem=ssem.at[kind, j], recv_sem=rsem.at[kind, j], device_id=dev, device_id_type=MESH
        )

    def arrived(ref, kind, j):
        remote(ref, ref, kind, j, {"ro": 1 - c}).wait_recv()

    def cols(j):
        return pl.ds(pl.multiple_of(j * LANES, LANES), LANES)

    def prow(is_full):
        return pl.ds(0, kb if is_full else half)

    qrow = pl.ds(half, kb - half)

    def flip(i, m, j):
        odd = lax.rem(j, 2)
        return lax.rem(i + m - 1 + 2 * odd, m), lax.rem(i + 1 + 2 * odd, m)

    def s0p(j, t):
        src, dst = w.at[prow(t), cols(j)], g.at[j, c, y, x, prow(t), :]
        remote(src, dst, P1L, j, {"co": xr}).start()
        remote(src, dst, P1R, j, {"co": xl}).start()

    def s1p(j, t):
        arrived(g.at[j, c, y, xl, prow(t), :], P1L, j)
        arrived(g.at[j, c, y, xr, prow(t), :], P1R, j)
        b, dev = flip(x, nx, j)
        ref = g.at[j, c, y, b, prow(t), :]
        remote(ref, ref, P1O, j, {"co": dev}).start()

    def s2p(j, t):
        arrived(g.at[j, c, y, xo, prow(t), :], P1O, j)
        ref = g.at[j, c, y, :, prow(t), :]
        remote(ref, ref, P2L, j, {"ri": yr}).start()
        remote(ref, ref, P2R, j, {"ri": yl}).start()

    def s3p(j, t):
        arrived(g.at[j, c, yl, :, prow(t), :], P2L, j)
        arrived(g.at[j, c, yr, :, prow(t), :], P2R, j)
        b, dev = flip(y, ny, j)
        ref = g.at[j, c, b, :, prow(t), :]
        remote(ref, ref, P2O, j, {"ri": dev}).start()

    def s4p(j, t):
        arrived(g.at[j, c, y, :, prow(t), :], P2O, j)

    def s0q(j):
        src, dst = w.at[qrow, cols(j)], g.at[j, c, y, x, qrow, :]
        remote(src, dst, Q1L, j, {"ri": yr}).start()
        remote(src, dst, Q1R, j, {"ri": yl}).start()

    def s1q(j):
        arrived(g.at[j, c, yl, x, qrow, :], Q1L, j)
        arrived(g.at[j, c, yr, x, qrow, :], Q1R, j)
        b, dev = flip(y, ny, j)
        ref = g.at[j, c, b, x, qrow, :]
        remote(ref, ref, Q1O, j, {"ri": dev}).start()

    def s2q(j):
        arrived(g.at[j, c, y, x, qrow, :], Q1O, j)
        ref = g.at[j, c, :, x, qrow, :]
        remote(ref, ref, Q2L, j, {"co": xr}).start()
        remote(ref, ref, Q2R, j, {"co": xl}).start()

    def s3q(j):
        arrived(g.at[j, c, :, xl, qrow, :], Q2L, j)
        arrived(g.at[j, c, :, xr, qrow, :], Q2R, j)
        b, dev = flip(x, nx, j)
        ref = g.at[j, c, :, b, qrow, :]
        remote(ref, ref, Q2O, j, {"co": dev}).start()

    def s4q(j):
        arrived(g.at[j, c, :, x, qrow, :], Q2O, j)

    def own(j):
        return pltpu.make_async_copy(w_v.at[:, cols(j)], g.at[j, c, y, x], lsem.at[j])

    def die(j):
        return remote(g.at[j, c], g.at[j, c], DIE, j, {"ro": 1 - c})

    def a_copy(i, k, dev):
        src = act.at[pl.ds(pl.multiple_of(dev * rows + k * apiece, apiece), apiece), :]
        dst = a_v.at[pl.ds(pl.multiple_of(k * apiece, apiece), apiece), pl.ds(pl.multiple_of(x * acols, acols), acols)]
        return pltpu.make_async_remote_copy(
            src_ref=src, dst_ref=dst, send_sem=a_ssem.at[i], recv_sem=a_rsem.at[i], device_id={"co": dev}, device_id_type=MESH
        )

    def a_all(i, src_x):
        ref = a_v.at[:, pl.ds(pl.multiple_of(src_x * acols, acols), acols)]
        return pltpu.make_async_remote_copy(
            src_ref=ref, dst_ref=ref, send_sem=a_ssem.at[i], recv_sem=a_rsem.at[i], device_id={"ro": 1 - c}, device_id_type=MESH
        )

    own_a = pltpu.make_async_copy(
        act.at[pl.ds(pl.multiple_of(x * rows, rows), rows), :], a_v.at[:, pl.ds(pl.multiple_of(x * acols, acols), acols)], lsem.at[n]
    )
    own_w = pltpu.make_async_copy(w, w_v, lsem.at[n + 1])

    def load(j, slot):
        return [
            pltpu.make_async_copy(g.at[j, :, :, i], b_v.at[slot, :, :, :, pl.ds(i * LANES, LANES)], bsem.at[slot, i])
            for i in range(nx)
        ]

    def store(j, slot):
        return [
            pltpu.make_async_copy(
                c_v.at[slot, :, pl.ds(i * LANES, LANES)],
                out.at[:, pl.ds(pl.multiple_of(i * wcols + j * LANES, LANES), LANES)],
                csem.at[slot, i],
            )
            for i in range(nx)
        ]

    def compute(slot):
        def tile(m, _):
            r = pl.ds(pl.multiple_of(m * 256, 256), 256)
            b = b_v[slot].reshape(kd, nx * LANES)
            c_v[slot, r, :] = jnp.dot(a_v[r, :], b, preferred_element_type=jnp.float32).astype(c_v.dtype)
            return 0

        lax.fori_loop(0, rows // 256, tile, 0)

    def step(i, _):
        slot = lax.rem(i, 2)

        @pl.when(i == 0)
        def _():
            own_a.wait()
            a_all(0, xl).wait_recv()
            a_all(1, xr).wait_recv()
            a_all(2, xo).wait_recv()

        @pl.when(i < n)
        def _():
            arrived(g.at[i, 1 - c], DIE, i)
            for cp in load(i, slot):
                cp.start()

        @pl.when(i >= 1)
        def _():
            for cp in load(i - 1, 1 - slot):
                cp.wait()

            @pl.when(i >= 3)
            def _():
                for cp in store(i - 3, 1 - slot):
                    cp.wait()

            compute(1 - slot)
            for cp in store(i - 1, 1 - slot):
                cp.start()

        return 0

    def by_type(j, stage):
        pl.when((j >= 0) & (j < full))(lambda: stage(j, True))
        pl.when((j >= full) & (j < n))(lambda: stage(j, False))

    def if_q(j, stage):
        pl.when((j >= full) & (j < n))(lambda: stage(j))

    own_w.start()
    own_a.start()
    own_w.wait()

    def start_own(j, _):
        own(j).start()
        return 0

    lead = 6
    c_start = 7

    def progress(r):
        return jnp.clip(jnp.minimum(2 * (r - c_start), r - 3), 0, n + 1)

    def turn(t, _):
        r = t - lead
        by_type(r + 6, s0p)
        if_q(r + full + 6, s0q)

        @pl.when(t == 0)
        def _():
            lax.fori_loop(0, n, start_own, 0)

        by_type(r + 4, s1p)
        if_q(r + full + 4, s1q)

        @pl.when((r >= -3) & (r < A_PIECES - 3))
        def _():
            for i, dev in enumerate((xr, xl, xo)):
                a_copy(i, r + 3, dev).start()

        @pl.when((r + 2 >= 0) & (r + 2 < n))
        def _():
            own(r + 2).wait()

        by_type(r + 2, s2p)
        if_q(r + 2, s2q)
        by_type(r, s3p)
        if_q(r, s3q)
        by_type(r - 2, s4p)
        if_q(r - 2, s4q)
        pl.when((r - 2 >= 0) & (r - 2 < n))(lambda: die(r - 2).start())
        lax.fori_loop(progress(r), progress(r + 1), step, 0)
        return 0

    lax.fori_loop(0, n + 4 + lead, turn, 0)

    for j in (n - 2, n - 1):
        for cp in store(j, j % 2):
            cp.wait()
    for i, src_x in enumerate((xl, xr, xo)):
        a_all(i, src_x).wait_send()

    def sent(j, _):
        def p(j, t):
            one, four = g.at[j, c, y, x, prow(t), :], g.at[j, c, y, :, prow(t), :]
            for kind in (P1L, P1R, P1O):
                remote(one, one, kind, j, {"ro": 1 - c}).wait_send()
            for kind in (P2L, P2R, P2O):
                remote(four, four, kind, j, {"ro": 1 - c}).wait_send()

        def q(j):
            one, four = g.at[j, c, y, x, qrow, :], g.at[j, c, :, x, qrow, :]
            for kind in (Q1L, Q1R, Q1O):
                remote(one, one, kind, j, {"ro": 1 - c}).wait_send()
            for kind in (Q2L, Q2R, Q2O):
                remote(four, four, kind, j, {"ro": 1 - c}).wait_send()

        by_type(j, p)
        if_q(j, q)
        die(j).wait_send()
        return 0

    lax.fori_loop(0, n, sent, 0)


def solution(mesh):
    nx, ny, nc = mesh.shape["co"], mesh.shape["ri"], mesh.shape["ro"]

    def local_block(act, w):
        kb, wcols = w.shape
        n = wcols // LANES
        rows, kd = act.shape[0] // nx, act.shape[1] * nx
        dt = act.dtype
        out, _ = pl.pallas_call(
            functools.partial(kernel, (nx, ny)),
            name="gather_matmul",
            out_shape=(
                jax.ShapeDtypeStruct((rows, wcols * nx), dt),
                jax.ShapeDtypeStruct((n, nc, ny, nx, kb, LANES), dt),
            ),
            in_specs=[pl.BlockSpec(memory_space=pl.ANY)] * 2,
            out_specs=(pl.BlockSpec(memory_space=pl.ANY),) * 2,
            scratch_shapes=[
                pltpu.VMEM((rows, kd), dt),
                pltpu.VMEM((kb, wcols), dt),
                pltpu.VMEM((2, nc, ny, kb, nx * LANES), dt),
                pltpu.VMEM((2, rows, nx * LANES), dt),
                pltpu.SemaphoreType.DMA((13, n)),
                pltpu.SemaphoreType.DMA((13, n)),
                pltpu.SemaphoreType.DMA((3,)),
                pltpu.SemaphoreType.DMA((3,)),
                pltpu.SemaphoreType.DMA((n + 2,)),
                pltpu.SemaphoreType.DMA((2, nx)),
                pltpu.SemaphoreType.DMA((2, nx)),
            ],
            compiler_params=pltpu.CompilerParams(collective_id=0, has_side_effects=True, vmem_limit_bytes=60 << 20),
        )(act, w)
        return out

    return jax.shard_map(
        local_block,
        mesh=mesh,
        in_specs=(P(("dp", "ro", "ri"), "co"), P(("ro", "ri"), "co")),
        out_specs=P(("dp", "ro", "ri", "co"), None),
        check_vma=False,
    )
```

time: 939 us -> 415 us (0.44)
  waiting for transfers between devices: 437 us -> 0 us
  Pallas kernels: 0 us -> 395 us
  blocking collectives: 335 us -> 0 us
  matrix products: 133 us -> 0 us
  between operations: 13.4 us -> 0.01 us
    all_gather x2 -> x0, waiting for transfers between devices: 436 us -> none  [the longest x1 296 us: local_block(): act_rows = lax.all_gather(act_blk, 'co', axis=1, tiled=True)]
    pallas_call x0 -> x1, Pallas kernels: none -> 395 us  [local_block(): pl.pallas_call(functools.partial(kernel, (nx, ny)), name='gather_matmul',...]
    all_to_all x1 -> x0, blocking collectives: 335 us -> none  [local_block(): return lax.all_to_all(block_out, 'co', 0, 1, tiled=True)]
    dot_general x1 -> x0, matrix products: 133 us -> none  [local_block(): jnp.dot(act_rows, weight_cols, preferred_element_type=jnp.float32)]
    all_to_all x1 -> x0, local copies, waits for them, and re-layouts: 20.4 us -> none  [local_block(): return lax.all_to_all(block_out, 'co', 0, 1, tiled=True)]
    unnamed x0 -> x1, local copies, waits for them, and re-layouts: none -> 20.1 us
  transfers between devices with their start and end apart: 2 -> 0, of which waited for: 2 -> 0; matrix products, arithmetic and copies ran while one was open for 0% -> 0% of each run, Pallas kernels for 0% -> 0%
where the time goes in v1:
time: 415 us
  Pallas kernels  395 us (95%)
  local copies, waits for them, and re-layouts  20.1 us (5%)
    pallas_call x1, Pallas kernels, local_block(): pl.pallas_call(functools.partial(kernel, (nx, ny)), name='gather_matmul',...  395 us
    unnamed x1, local copies, waits for them, and re-layouts  20.1 us

profile of v1, /device:TPU:97, one launch (start us, length us, event | category | flops | bytes accessed | tf_op | source)
XLA Modules:
  0.0 414.9 jit_solution(17817254547562007370)
XLA Ops:
  0.0 394.7 %gather_matmul.1 = (bf16[1024,14336]{1,0:T(8,128)(2,1)}, bf16[28,2,4,4,512,128]{5,4,3,2,1,0:T(8,128)(2,1)}) custom-call(bf16[4096,1024]{1,0:T(8,128)(2,1)} %act.1, bf16[512,3584]{1,0:T(8,128)(2,1)} %w.1), custom_call_target="tpu_custom_call" | custom-call | tf_op jit(solution)/shard_map/gather_matmul/pallas_call | solution.py:284
  394.7 20.1 %copy.4 = bf16[1024,14336]{1,0:T(8,128)(2,1)} copy(bf16[1024,14336]{1,0:T(8,128)(2,1)} %get-tuple-element.6) | data formatting | bytes 58720256

commit v2 on v1

v2 whole, which is shorter than its diff:
```python
import functools

import jax
import jax.numpy as jnp
from jax import lax
from jax.experimental import pallas as pl
from jax.experimental.pallas import tpu as pltpu
from jax.sharding import PartitionSpec as P

MESH = pl.DeviceIdType.MESH
LANES = 128
A_PIECES = 8
FIN = 2
TILE = 512
C_PARTS = 8
P1L, P1R, P1U, P1D, P2L, P2R, P2U, P2D, Q1L, Q1R, Q1U, Q1D, Q2L, Q2R, Q2U, Q2D, DIE = range(17)


def kernel(dims, act, w, a_v, b_v, c_v, g, w_v, rsem, ssem, a_rsem, a_ssem, lsem, bsem):
    nx, ny = dims
    kb, wcols = w.shape
    n = wcols // LANES
    nc = n - FIN
    full = n // 4
    half = kb // 2
    rows, kd = a_v.shape
    acols = kd // nx
    apiece = rows // A_PIECES

    x, y, c = lax.axis_index("co"), lax.axis_index("ri"), lax.axis_index("ro")
    xl, xr, xo = lax.rem(x + nx - 1, nx), lax.rem(x + 1, nx), lax.rem(x + 2, nx)
    yl, yr, yo = lax.rem(y + ny - 1, ny), lax.rem(y + 1, ny), lax.rem(y + 2, ny)

    barrier = pltpu.get_barrier_semaphore()
    peers = [{"co": xl}, {"co": xr}, {"co": xo}, {"ri": yl}, {"ri": yr}, {"ro": 1 - c}]
    for peer in peers:
        pl.semaphore_signal(barrier, inc=1, device_id=peer, device_id_type=MESH)
    pl.semaphore_wait(barrier, len(peers))

    def remote(src, dst, kind, j, dev):
        return pltpu.make_async_remote_copy(
            src_ref=src, dst_ref=dst, send_sem=ssem.at[kind, j], recv_sem=rsem.at[kind, j], device_id=dev, device_id_type=MESH
        )

    def arrived(ref, kind, j):
        remote(ref, ref, kind, j, {"ro": 1 - c}).wait_recv()

    def cols(j):
        return pl.ds(pl.multiple_of(j * LANES, LANES), LANES)

    def prow(is_full, part=0):
        size = kb if is_full else half
        return (pl.ds(0, size), pl.ds(0, size // 2), pl.ds(size // 2, size // 2))[part]

    def qrow(part=0):
        size = kb - half
        return (pl.ds(half, size), pl.ds(half, size // 2), pl.ds(half + size // 2, size // 2))[part]

    def s0p(j, t):
        src, dst = w.at[prow(t), cols(j)], g.at[j, c, y, x, prow(t), :]
        remote(src, dst, P1L, j, {"co": xr}).start()
        remote(src, dst, P1R, j, {"co": xl}).start()

    def s1p(j, t):
        arrived(g.at[j, c, y, xl, prow(t), :], P1L, j)
        up = g.at[j, c, y, xl, prow(t, 1), :]
        remote(up, up, P1U, j, {"co": xr}).start()
        arrived(g.at[j, c, y, xr, prow(t), :], P1R, j)
        down = g.at[j, c, y, xr, prow(t, 2), :]
        remote(down, down, P1D, j, {"co": xl}).start()

    def s2p(j, t):
        arrived(g.at[j, c, y, xo, prow(t, 1), :], P1U, j)
        arrived(g.at[j, c, y, xo, prow(t, 2), :], P1D, j)
        ref = g.at[j, c, y, :, prow(t), :]
        remote(ref, ref, P2L, j, {"ri": yr}).start()
        remote(ref, ref, P2R, j, {"ri": yl}).start()

    def s3p(j, t):
        arrived(g.at[j, c, yl, :, prow(t), :], P2L, j)
        up = g.at[j, c, yl, :, prow(t, 1), :]
        remote(up, up, P2U, j, {"ri": yr}).start()
        arrived(g.at[j, c, yr, :, prow(t), :], P2R, j)
        down = g.at[j, c, yr, :, prow(t, 2), :]
        remote(down, down, P2D, j, {"ri": yl}).start()

    def s4p(j, t):
        arrived(g.at[j, c, yo, :, prow(t, 1), :], P2U, j)
        arrived(g.at[j, c, yo, :, prow(t, 2), :], P2D, j)

    def s0q(j):
        src, dst = w.at[qrow(), cols(j)], g.at[j, c, y, x, qrow(), :]
        remote(src, dst, Q1L, j, {"ri": yr}).start()
        remote(src, dst, Q1R, j, {"ri": yl}).start()

    def s1q(j):
        arrived(g.at[j, c, yl, x, qrow(), :], Q1L, j)
        up = g.at[j, c, yl, x, qrow(1), :]
        remote(up, up, Q1U, j, {"ri": yr}).start()
        arrived(g.at[j, c, yr, x, qrow(), :], Q1R, j)
        down = g.at[j, c, yr, x, qrow(2), :]
        remote(down, down, Q1D, j, {"ri": yl}).start()

    def s2q(j):
        arrived(g.at[j, c, yo, x, qrow(1), :], Q1U, j)
        arrived(g.at[j, c, yo, x, qrow(2), :], Q1D, j)
        ref = g.at[j, c, :, x, qrow(), :]
        remote(ref, ref, Q2L, j, {"co": xr}).start()
        remote(ref, ref, Q2R, j, {"co": xl}).start()

    def s3q(j):
        arrived(g.at[j, c, :, xl, qrow(), :], Q2L, j)
        up = g.at[j, c, :, xl, qrow(1), :]
        remote(up, up, Q2U, j, {"co": xr}).start()
        arrived(g.at[j, c, :, xr, qrow(), :], Q2R, j)
        down = g.at[j, c, :, xr, qrow(2), :]
        remote(down, down, Q2D, j, {"co": xl}).start()

    def s4q(j):
        arrived(g.at[j, c, :, xo, qrow(1), :], Q2U, j)
        arrived(g.at[j, c, :, xo, qrow(2), :], Q2D, j)

    def own(j):
        return pltpu.make_async_copy(w_v.at[:, cols(j)], g.at[j, c, y, x], lsem.at[j])

    def die(j):
        return remote(g.at[j, c], g.at[j, c], DIE, j, {"ro": 1 - c})

    def a_copy(i, k, dev):
        src = act.at[pl.ds(pl.multiple_of(dev * rows + k * apiece, apiece), apiece), :]
        dst = a_v.at[pl.ds(pl.multiple_of(k * apiece, apiece), apiece), pl.ds(pl.multiple_of(x * acols, acols), acols)]
        return pltpu.make_async_remote_copy(
            src_ref=src, dst_ref=dst, send_sem=a_ssem.at[i], recv_sem=a_rsem.at[i], device_id={"co": dev}, device_id_type=MESH
        )

    def a_all(i, src_x):
        ref = a_v.at[:, pl.ds(pl.multiple_of(src_x * acols, acols), acols)]
        return pltpu.make_async_remote_copy(
            src_ref=ref, dst_ref=ref, send_sem=a_ssem.at[i], recv_sem=a_rsem.at[i], device_id={"ro": 1 - c}, device_id_type=MESH
        )

    own_a = pltpu.make_async_copy(
        act.at[pl.ds(pl.multiple_of(x * rows, rows), rows), :], a_v.at[:, pl.ds(pl.multiple_of(x * acols, acols), acols)], lsem.at[n]
    )
    own_w = pltpu.make_async_copy(w, w_v, lsem.at[n + 1])

    def load(j, slot):
        return loads(g, b_v, bsem, j, slot)

    def step(i, _):
        slot = lax.rem(i, 2)

        @pl.when(i == 0)
        def _():
            own_a.wait()
            a_all(0, xl).wait_recv()
            a_all(1, xr).wait_recv()
            a_all(2, xo).wait_recv()

        @pl.when(i <= nc)
        def _():
            arrived(g.at[i, 1 - c], DIE, i)
            for cp in load(i, slot):
                cp.start()

        @pl.when(i >= 1)
        def _():
            for cp in load(i - 1, 1 - slot):
                cp.wait()
            multiply(a_v, b_v.at[1 - slot], c_v, i - 1)

        return 0

    def by_type(j, stage):
        pl.when((j >= 0) & (j < full))(lambda: stage(j, True))
        pl.when((j >= full) & (j < n))(lambda: stage(j, False))

    def if_q(j, stage):
        pl.when((j >= full) & (j < n))(lambda: stage(j))

    own_w.start()
    own_a.start()

    def start_own(j, _):
        own(j).start()
        return 0

    gap = 3
    lead = 3 * gap
    c_start = 7
    a_start = 3

    def finished(r):
        return jnp.clip(jnp.where(r <= n, r - gap, 2 * r - n - gap), 0, n)

    def progress(r):
        return jnp.clip(jnp.minimum(2 * (r - c_start), r - gap - 1), 0, nc + 1)

    def last_hop(j, _):
        by_type(j, s4p)
        if_q(j, s4q)

        @pl.when(j < n - 1)
        def _():
            die(j).start()

        @pl.when(j == n - 1)
        def _():
            die_part(g.at[j, c, yo, :, prow(False), :]).start()
            die_part(g.at[j, c, :, xo, qrow(), :]).start()

        return 0

    def die_part(ref):
        return remote(ref, ref, DIE, n - 1, {"ro": 1 - c})

    def turn(t, _):
        r = t - lead
        by_type(r + 3 * gap, s0p)
        if_q(r + full + 3 * gap, s0q)

        @pl.when(t == 0)
        def _():
            own_w.wait()
            lax.fori_loop(0, n, start_own, 0)

        by_type(r + 2 * gap, s1p)
        if_q(r + full + 2 * gap, s1q)

        @pl.when((r >= -a_start) & (r < A_PIECES - a_start))
        def _():
            for i, dev in enumerate((xr, xl, xo)):
                a_copy(i, r + a_start, dev).start()

        @pl.when((r + gap >= 0) & (r + gap < n))
        def _():
            own(r + gap).wait()

        by_type(r + gap, s2p)
        if_q(r + gap, s2q)
        j3 = jnp.where(r == n - 1, n, jnp.where(r == n, n - 1, r))
        by_type(j3, s3p)
        if_q(j3, s3q)

        @pl.when(j3 == n - 1)
        def _():
            for b in (y, yl, yr):
                die_part(g.at[j3, c, b, :, prow(False), :]).start()
            for b in (x, xl, xr):
                die_part(g.at[j3, c, :, b, qrow(), :]).start()

        lax.fori_loop(finished(r), finished(r + 1), last_hop, 0)
        lax.fori_loop(progress(r), progress(r + 1), step, 0)
        return 0

    lax.fori_loop(0, nc + gap + 2 + lead, turn, 0)

    for cp in load(nc, nc % 2):
        cp.wait()
    arrived(g.at[n - 1, 1 - c], DIE, n - 1)
    for i, src_x in enumerate((xl, xr, xo)):
        a_all(i, src_x).wait_send()

    def sent(j, _):
        def p(j, t):
            for kind, ref in (
                (P1L, g.at[j, c, y, x, prow(t), :]),
                (P1R, g.at[j, c, y, x, prow(t), :]),
                (P1U, g.at[j, c, y, x, prow(t, 1), :]),
                (P1D, g.at[j, c, y, x, prow(t, 2), :]),
                (P2L, g.at[j, c, y, :, prow(t), :]),
                (P2R, g.at[j, c, y, :, prow(t), :]),
                (P2U, g.at[j, c, y, :, prow(t, 1), :]),
                (P2D, g.at[j, c, y, :, prow(t, 2), :]),
            ):
                remote(ref, ref, kind, j, {"ro": 1 - c}).wait_send()

        def q(j):
            for kind, ref in (
                (Q1L, g.at[j, c, y, x, qrow(), :]),
                (Q1R, g.at[j, c, y, x, qrow(), :]),
                (Q1U, g.at[j, c, y, x, qrow(1), :]),
                (Q1D, g.at[j, c, y, x, qrow(2), :]),
                (Q2L, g.at[j, c, :, x, qrow(), :]),
                (Q2R, g.at[j, c, :, x, qrow(), :]),
                (Q2U, g.at[j, c, :, x, qrow(1), :]),
                (Q2D, g.at[j, c, :, x, qrow(2), :]),
            ):
                remote(ref, ref, kind, j, {"ro": 1 - c}).wait_send()

        by_type(j, p)
        if_q(j, q)
        die(j).wait_send()
        return 0

    lax.fori_loop(0, n, sent, 0)


def loads(g, b_v, sem, j, slot):
    return [
        pltpu.make_async_copy(g.at[j, :, :, i], b_v.at[slot, :, :, :, pl.ds(i * LANES, LANES)], sem.at[slot, i])
        for i in range(g.shape[3])
    ]


def multiply(a_v, b, c_v, j):
    nx = b.shape[-1] // LANES
    width = c_v.shape[-1] // nx

    def tile(m, _):
        r = pl.ds(pl.multiple_of(m * TILE, TILE), TILE)
        c = jnp.dot(a_v[r, :], b[...].reshape(a_v.shape[-1], nx * LANES), preferred_element_type=jnp.float32)
        for i in range(nx):
            col = pl.ds(pl.multiple_of(i * width + j * LANES, LANES), LANES)
            c_v[r, col] = c[:, i * LANES : (i + 1) * LANES].astype(c_v.dtype)
        return 0

    lax.fori_loop(0, a_v.shape[0] // TILE, tile, 0)


def finish(a_v, b_v, c_v, g, out, last_v, d_v, bsem, csem, dsem):
    n, _, _, nx, _, _ = g.shape
    rows, nc = c_v.shape[0], n - FIN
    part = rows // C_PARTS

    def stores(ref, first, count, sem):
        width = count * LANES
        cps = []
        for k in range(C_PARTS):
            for i in range(nx):
                r = pl.ds(k * part, part)
                dst = out.at[r, pl.ds(i * n * LANES + first * LANES, width)]
                cps.append(pltpu.make_async_copy(ref.at[r, pl.ds(i * width, width)], dst, sem.at[k, i]))
        return cps

    for cp in loads(g, last_v, bsem, n - 1, 0):
        cp.start()
    for cp in stores(c_v, 0, nc, csem):
        cp.start()

    multiply(a_v, b_v.at[nc % 2], d_v, 0)
    for cp in loads(g, last_v, bsem, n - 1, 0):
        cp.wait()
    multiply(a_v, last_v.at[0], d_v, 1)
    for cp in stores(d_v, nc, FIN, dsem):
        cp.start()
    for cp in stores(c_v, 0, nc, csem) + stores(d_v, nc, FIN, dsem):
        cp.wait()


def solution(mesh):
    nx, ny, ncore = mesh.shape["co"], mesh.shape["ri"], mesh.shape["ro"]

    def local_block(act, w):
        kb, wcols = w.shape
        n = wcols // LANES
        rows, kd = act.shape[0] // nx, act.shape[1] * nx
        dt = act.dtype
        wide = nx * LANES
        any_spec = pl.BlockSpec(memory_space=pl.ANY)
        vmem_spec = pl.BlockSpec(memory_space=pltpu.VMEM)
        a_v, b_v, c_v, g = pl.pallas_call(
            functools.partial(kernel, (nx, ny)),
            name="gather_matmul",
            out_shape=(
                pltpu.VMEM((rows, kd), dt),
                pltpu.VMEM((2, ncore, ny, kb, wide), dt),
                pltpu.VMEM((rows, wide * (n - FIN)), dt),
                jax.ShapeDtypeStruct((n, ncore, ny, nx, kb, LANES), dt),
            ),
            in_specs=[any_spec] * 2,
            out_specs=(vmem_spec, vmem_spec, vmem_spec, any_spec),
            scratch_shapes=[
                pltpu.VMEM((kb, wcols), dt),
                pltpu.SemaphoreType.DMA((17, n)),
                pltpu.SemaphoreType.DMA((17, n)),
                pltpu.SemaphoreType.DMA((3,)),
                pltpu.SemaphoreType.DMA((3,)),
                pltpu.SemaphoreType.DMA((n + 2,)),
                pltpu.SemaphoreType.DMA((2, nx)),
            ],
            compiler_params=pltpu.CompilerParams(collective_id=0, has_side_effects=True, vmem_limit_bytes=12 << 20),
        )(act, w)
        held = [pltpu.with_memory_space_constraint(v, pltpu.VMEM) for v in (a_v, b_v, c_v)]
        return pl.pallas_call(
            finish,
            name="finish",
            out_shape=jax.ShapeDtypeStruct((rows, wcols * nx), dt),
            in_specs=[vmem_spec] * 3 + [any_spec],
            out_specs=any_spec,
            scratch_shapes=[
                pltpu.VMEM((1, ncore, ny, kb, wide), dt),
                pltpu.VMEM((rows, wide * FIN), dt),
                pltpu.SemaphoreType.DMA((1, nx)),
                pltpu.SemaphoreType.DMA((C_PARTS, nx)),
                pltpu.SemaphoreType.DMA((C_PARTS, nx)),
            ],
            compiler_params=pltpu.CompilerParams(vmem_limit_bytes=12 << 20),
        )(*held, g)

    return jax.shard_map(
        local_block,
        mesh=mesh,
        in_specs=(P(("dp", "ro", "ri"), "co"), P(("ro", "ri"), "co")),
        out_specs=P(("dp", "ro", "ri", "co"), None),
        check_vma=False,
    )
```

time: 415 us -> 386 us (0.930)
  local copies, waits for them, and re-layouts: 20.1 us -> 0 us
  Pallas kernels: 395 us -> 386 us
    pallas_call x1, Pallas kernels: 395 us -> 374 us  [local_block(): pl.pallas_call(functools.partial(kernel, (nx, ny)), name='gather_matmul',...]
    unnamed x1 -> x0, local copies, waits for them, and re-layouts: 20.1 us -> none
    pallas_call x0 -> x1, Pallas kernels: none -> 11.7 us  [local_block(): pl.pallas_call(finish, name='finish', out_shape=jax.ShapeDtypeStruct((row...]
where the time goes in v2:
time: 386 us
  Pallas kernels  386 us (100%)
    pallas_call x1, Pallas kernels, local_block(): pl.pallas_call(functools.partial(kernel, (nx, ny)), name='gather_matmul',...  374 us
    pallas_call x1, Pallas kernels, local_block(): pl.pallas_call(finish, name='finish', out_shape=jax.ShapeDtypeStruct((row...  11.7 us

profile of v2, /device:TPU:97, one launch (start us, length us, event | category | flops | bytes accessed | tf_op | source)
XLA Modules:
  0.0 386.0 jit_solution(12070739108118375976)
XLA Ops:
  0.0 374.3 %gather_matmul.1 = (bf16[1024,4096]{1,0:T(8,128)(2,1)S(1)}, bf16[2,2,4,512,512]{4,3,2,1,0:T(8,128)(2,1)S(1)}, bf16[1024,13312]{1,0:T(8,128)(2,1)S(1)}, bf16[28,2,4,4,512,128]{5,4,3,2,1,0:T(8,128)(2,1)}) custom-call(bf16[4096,1024]{1,0:T(8,128)(2,1)} %act.1, bf16[512,3584]{1,0:T(8,128)(2,1)} %w.1), custom_call_target="tpu_custom_call" | custom-call | tf_op jit(solution)/shard_map/gather_matmul/pallas_call | solution.py:362
  374.3 11.7 %finish.1 = bf16[1024,14336]{1,0:T(8,128)(2,1)} custom-call(bf16[1024,4096]{1,0:T(8,128)(2,1)S(1)} %get-tuple-element.9.a_v, bf16[2,2,4,512,512]{4,3,2,1,0:T(8,128)(2,1)S(1)} %get-tuple-element.10.b_v, bf16[1024,13312]{1,0:T(8,128)(2,1)S(1)} %get-tuple-element.11.c_v, bf16[28,2,4,4,512,128]{5,4,3,2,1,0:T(8,128)(2,1)} %get-tuple-element.12.g), custom_call_target="tpu_custom_call" | custom-call | tf_op jit(solution)/shard_map/finish/pallas_call | solution.py:385

commit v3 on v2

--- a/solution.py
+++ b/solution.py
@@ -12,7 +12,7 @@
 A_PIECES = 8
 FIN = 2
 TILE = 512
-C_PARTS = 8
+C_PARTS = 4
 P1L, P1R, P1U, P1D, P2L, P2R, P2U, P2D, Q1L, Q1R, Q1U, Q1D, Q2L, Q2R, Q2U, Q2D, DIE = range(17)
 
 
@@ -147,7 +147,13 @@
     def load(j, slot):
         return loads(g, b_v, bsem, j, slot)
 
-    def step(i, _):
+    def fetch(i, _):
+        arrived(g.at[i, 1 - c], DIE, i)
+        for cp in load(i, lax.rem(i, 2)):
+            cp.start()
+        return 0
+
+    def use(i, _):
         slot = lax.rem(i, 2)
 
         @pl.when(i == 0)
@@ -157,18 +163,13 @@
             a_all(1, xr).wait_recv()
             a_all(2, xo).wait_recv()
 
-        @pl.when(i <= nc)
-        def _():
-            arrived(g.at[i, 1 - c], DIE, i)
-            for cp in load(i, slot):
-                cp.start()
-
-        @pl.when(i >= 1)
-        def _():
-            for cp in load(i - 1, 1 - slot):
-                cp.wait()
-            multiply(a_v, b_v.at[1 - slot], c_v, i - 1)
-
+        @pl.when(i == nc - 1)
+        def _():
+            fetch(nc, 0)
+
+        for cp in load(i, slot):
+            cp.wait()
+        multiply(a_v, b_v.at[slot], c_v, i)
         return 0
 
     def by_type(j, stage):
@@ -194,28 +195,35 @@
         return jnp.clip(jnp.where(r <= n, r - gap, 2 * r - n - gap), 0, n)
 
     def progress(r):
-        return jnp.clip(jnp.minimum(2 * (r - c_start), r - gap - 1), 0, nc + 1)
+        return jnp.clip(jnp.minimum(2 * (r - c_start), r - gap - 1), 0, nc)
 
     def last_hop(j, _):
         by_type(j, s4p)
         if_q(j, s4q)
 
-        @pl.when(j < n - 1)
+        @pl.when(j < full)
         def _():
             die(j).start()
 
-        @pl.when(j == n - 1)
-        def _():
-            die_part(g.at[j, c, yo, :, prow(False), :]).start()
-            die_part(g.at[j, c, :, xo, qrow(), :]).start()
-
-        return 0
-
-    def die_part(ref):
-        return remote(ref, ref, DIE, n - 1, {"ro": 1 - c})
+        @pl.when(j >= full)
+        def _():
+            die_part(j, g.at[j, c, yo, :, prow(False), :])
+            die_part(j, g.at[j, c, :, xo, qrow(), :])
+
+        return 0
+
+    def die_part(j, ref):
+        remote(ref, ref, DIE, j, {"ro": 1 - c}).start()
+
+    def die_early(j):
+        for b in (y, yl, yr):
+            die_part(j, g.at[j, c, b, :, prow(False), :])
+        for b in (x, xl, xr):
+            die_part(j, g.at[j, c, :, b, qrow(), :])
 
     def turn(t, _):
         r = t - lead
+        lax.fori_loop(progress(r), progress(r + 1), fetch, 0)
         by_type(r + 3 * gap, s0p)
         if_q(r + full + 3 * gap, s0q)
 
@@ -238,22 +246,14 @@
 
         by_type(r + gap, s2p)
         if_q(r + gap, s2q)
-        j3 = jnp.where(r == n - 1, n, jnp.where(r == n, n - 1, r))
-        by_type(j3, s3p)
-        if_q(j3, s3q)
-
-        @pl.when(j3 == n - 1)
-        def _():
-            for b in (y, yl, yr):
-                die_part(g.at[j3, c, b, :, prow(False), :]).start()
-            for b in (x, xl, xr):
-                die_part(g.at[j3, c, :, b, qrow(), :]).start()
-
+        by_type(r, s3p)
+        if_q(r, s3q)
+        if_q(r, die_early)
         lax.fori_loop(finished(r), finished(r + 1), last_hop, 0)
-        lax.fori_loop(progress(r), progress(r + 1), step, 0)
-        return 0
-
-    lax.fori_loop(0, nc + gap + 2 + lead, turn, 0)
+        lax.fori_loop(progress(r), progress(r + 1), use, 0)
+        return 0
+
+    lax.fori_loop(0, nc + gap + 1 + lead, turn, 0)
 
     for cp in load(nc, nc % 2):
         cp.wait()
@@ -303,16 +303,19 @@
     ]
 
 
-def multiply(a_v, b, c_v, j):
+def multiply_rows(a_v, b, c_v, j, m):
     nx = b.shape[-1] // LANES
     width = c_v.shape[-1] // nx
-
+    r = pl.ds(pl.multiple_of(m * TILE, TILE), TILE)
+    c = jnp.dot(a_v[r, :], b[...].reshape(a_v.shape[-1], nx * LANES), preferred_element_type=jnp.float32)
+    for i in range(nx):
+        col = pl.ds(pl.multiple_of(i * width + j * LANES, LANES), LANES)
+        c_v[r, col] = c[:, i * LANES : (i + 1) * LANES].astype(c_v.dtype)
+
+
+def multiply(a_v, b, c_v, j):
     def tile(m, _):
-        r = pl.ds(pl.multiple_of(m * TILE, TILE), TILE)
-        c = jnp.dot(a_v[r, :], b[...].reshape(a_v.shape[-1], nx * LANES), preferred_element_type=jnp.float32)
-        for i in range(nx):
-            col = pl.ds(pl.multiple_of(i * width + j * LANES, LANES), LANES)
-            c_v[r, col] = c[:, i * LANES : (i + 1) * LANES].astype(c_v.dtype)
+        multiply_rows(a_v, b, c_v, j, m)
         return 0
 
     lax.fori_loop(0, a_v.shape[0] // TILE, tile, 0)
@@ -321,31 +324,39 @@
 def finish(a_v, b_v, c_v, g, out, last_v, d_v, bsem, csem, dsem):
     n, _, _, nx, _, _ = g.shape
     rows, nc = c_v.shape[0], n - FIN
-    part = rows // C_PARTS
-
-    def stores(ref, first, count, sem):
+
+    def stores(ref, first, count, k, size, sem):
         width = count * LANES
-        cps = []
-        for k in range(C_PARTS):
-            for i in range(nx):
-                r = pl.ds(k * part, part)
-                dst = out.at[r, pl.ds(i * n * LANES + first * LANES, width)]
-                cps.append(pltpu.make_async_copy(ref.at[r, pl.ds(i * width, width)], dst, sem.at[k, i]))
-        return cps
-
+        r = pl.ds(pl.multiple_of(k * size, size), size)
+        return [
+            pltpu.make_async_copy(
+                ref.at[r, pl.ds(i * width, width)], out.at[r, pl.ds((i * n + first) * LANES, width)], sem.at[k, i]
+            )
+            for i in range(nx)
+        ]
+
+    held = [cp for k in range(C_PARTS) for cp in stores(c_v, 0, nc, k, rows // C_PARTS, csem)]
     for cp in loads(g, last_v, bsem, n - 1, 0):
         cp.start()
-    for cp in stores(c_v, 0, nc, csem):
+    for cp in held:
         cp.start()
 
     multiply(a_v, b_v.at[nc % 2], d_v, 0)
     for cp in loads(g, last_v, bsem, n - 1, 0):
         cp.wait()
-    multiply(a_v, last_v.at[0], d_v, 1)
-    for cp in stores(d_v, nc, FIN, dsem):
-        cp.start()
-    for cp in stores(c_v, 0, nc, csem) + stores(d_v, nc, FIN, dsem):
+
+    def tile(m, _):
+        multiply_rows(a_v, last_v.at[0], d_v, 1, m)
+        for cp in stores(d_v, nc, FIN, m, TILE, dsem):
+            cp.start()
+        return 0
+
+    lax.fori_loop(0, rows // TILE, tile, 0)
+    for cp in held:
         cp.wait()
+    for m in range(rows // TILE):
+        for cp in stores(d_v, nc, FIN, m, TILE, dsem):
+            cp.wait()
 
 
 def solution(mesh):
@@ -393,7 +404,7 @@
                 pltpu.VMEM((rows, wide * FIN), dt),
                 pltpu.SemaphoreType.DMA((1, nx)),
                 pltpu.SemaphoreType.DMA((C_PARTS, nx)),
-                pltpu.SemaphoreType.DMA((C_PARTS, nx)),
+                pltpu.SemaphoreType.DMA((rows // TILE, nx)),
             ],
             compiler_params=pltpu.CompilerParams(vmem_limit_bytes=12 << 20),
         )(*held, g)

time: 386 us -> 382 us (0.990)
  Pallas kernels: 386 us -> 381 us
    pallas_call x1, Pallas kernels: 374 us -> 370 us  [local_block(): pl.pallas_call(functools.partial(kernel, (nx, ny)), name='gather_matmul',...]
where the time goes in v3:
time: 382 us; the launch traced here: 381 us
  Pallas kernels  381 us (100%)
    pallas_call x1, Pallas kernels, local_block(): pl.pallas_call(functools.partial(kernel, (nx, ny)), name='gather_matmul',...  370 us
    pallas_call x1, Pallas kernels, local_block(): pl.pallas_call(finish, name='finish', out_shape=jax.ShapeDtypeStruct((row...  11 us

profile of v3, /device:TPU:97, one launch (start us, length us, event | category | flops | bytes accessed | tf_op | source)
XLA Modules:
  0.0 380.9 jit_solution(782725219508109191)
XLA Ops:
  0.0 369.8 %gather_matmul.1 = (bf16[1024,4096]{1,0:T(8,128)(2,1)S(1)}, bf16[2,2,4,512,512]{4,3,2,1,0:T(8,128)(2,1)S(1)}, bf16[1024,13312]{1,0:T(8,128)(2,1)S(1)}, bf16[28,2,4,4,512,128]{5,4,3,2,1,0:T(8,128)(2,1)}) custom-call(bf16[4096,1024]{1,0:T(8,128)(2,1)} %act.1, bf16[512,3584]{1,0:T(8,128)(2,1)} %w.1), custom_call_target="tpu_custom_call" | custom-call | tf_op jit(solution)/shard_map/gather_matmul/pallas_call | solution.py:373
  369.8 11.0 %finish.1 = bf16[1024,14336]{1,0:T(8,128)(2,1)} custom-call(bf16[1024,4096]{1,0:T(8,128)(2,1)S(1)} %get-tuple-element.9.a_v, bf16[2,2,4,512,512]{4,3,2,1,0:T(8,128)(2,1)S(1)} %get-tuple-element.10.b_v, bf16[1024,13312]{1,0:T(8,128)(2,1)S(1)} %get-tuple-element.11.c_v, bf16[28,2,4,4,512,128]{5,4,3,2,1,0:T(8,128)(2,1)} %get-tuple-element.12.g), custom_call_target="tpu_custom_call" | custom-call | tf_op jit(solution)/shard_map/finish/pallas_call | solution.py:396

commit v4 on v3

--- a/solution.py
+++ b/solution.py
@@ -11,6 +11,7 @@
 LANES = 128
 A_PIECES = 8
 FIN = 2
+AHEAD = 2
 TILE = 512
 C_PARTS = 4
 P1L, P1R, P1U, P1D, P2L, P2R, P2U, P2D, Q1L, Q1R, Q1U, Q1D, Q2L, Q2R, Q2U, Q2D, DIE = range(17)
@@ -163,12 +164,13 @@
             a_all(1, xr).wait_recv()
             a_all(2, xo).wait_recv()
 
-        @pl.when(i == nc - 1)
-        def _():
-            fetch(nc, 0)
-
         for cp in load(i, slot):
             cp.wait()
+
+        @pl.when(i >= nc - AHEAD)
+        def _():
+            fetch(i + 1, 0)
+
         multiply(a_v, b_v.at[slot], c_v, i)
         return 0
 
@@ -189,6 +191,7 @@
     gap = 3
     lead = 3 * gap
     c_start = 7
+    early = nc - AHEAD + 1
     a_start = 3
 
     def finished(r):
@@ -223,7 +226,7 @@
 
     def turn(t, _):
         r = t - lead
-        lax.fori_loop(progress(r), progress(r + 1), fetch, 0)
+        lax.fori_loop(jnp.minimum(progress(r), early), jnp.minimum(progress(r + 1), early), fetch, 0)
         by_type(r + 3 * gap, s0p)
         if_q(r + full + 3 * gap, s0q)
 

time: 382 us -> 381 us (level)
  no operation moved by 1% of the time
where the time goes in v4:
time: 381 us
  Pallas kernels  381 us (100%)
    pallas_call x1, Pallas kernels, local_block(): pl.pallas_call(functools.partial(kernel, (nx, ny)), name='gather_matmul',...  370 us
    pallas_call x1, Pallas kernels, local_block(): pl.pallas_call(finish, name='finish', out_shape=jax.ShapeDtypeStruct((row...  11 us

profile of v4, /device:TPU:97, one launch (start us, length us, event | category | flops | bytes accessed | tf_op | source)
XLA Modules:
  0.0 380.9 jit_solution(8319030045163443396)
XLA Ops:
  0.0 369.8 %gather_matmul.1 = (bf16[1024,4096]{1,0:T(8,128)(2,1)S(1)}, bf16[2,2,4,512,512]{4,3,2,1,0:T(8,128)(2,1)S(1)}, bf16[1024,13312]{1,0:T(8,128)(2,1)S(1)}, bf16[28,2,4,4,512,128]{5,4,3,2,1,0:T(8,128)(2,1)}) custom-call(bf16[4096,1024]{1,0:T(8,128)(2,1)} %act.1, bf16[512,3584]{1,0:T(8,128)(2,1)} %w.1), custom_call_target="tpu_custom_call" | custom-call | tf_op jit(solution)/shard_map/gather_matmul/pallas_call | solution.py:376
  369.8 11.0 %finish.1 = bf16[1024,14336]{1,0:T(8,128)(2,1)} custom-call(bf16[1024,4096]{1,0:T(8,128)(2,1)S(1)} %get-tuple-element.9.a_v, bf16[2,2,4,512,512]{4,3,2,1,0:T(8,128)(2,1)S(1)} %get-tuple-element.10.b_v, bf16[1024,13312]{1,0:T(8,128)(2,1)S(1)} %get-tuple-element.11.c_v, bf16[28,2,4,4,512,128]{5,4,3,2,1,0:T(8,128)(2,1)} %get-tuple-element.12.g), custom_call_target="tpu_custom_call" | custom-call | tf_op jit(solution)/shard_map/finish/pallas_call | solution.py:399
